TPU v7x, 32 devices: a whole 2x2x4 slice. The times are simulated.
32 devices in a mesh: dp: 8 (over z, core), tensor: 4 (over y, x).
Axes of the slice: x: 2, y: 2, z: 4, core: 2. Of those that a mesh axis runs over, the one named last changes fastest.
Arguments:
- tokens: bfloat16 [10240, 4096], P(('dp', 'tensor')), parts along dimension 0, may hold values from -6 to 6
- norm_gain: bfloat16 [4096], replicated, may hold values from 0.099609375 to 1.8984375
- query_weight: bfloat16 [4096, 8192], P(None, 'tensor'), may hold values from -0.09375 to 0.09375
- key_weight: bfloat16 [4096, 1024], P(None, 'tensor'), may hold values from -0.09375 to 0.09375
- value_weight: bfloat16 [4096, 1024], P(None, 'tensor'), may hold values from -0.09375 to 0.09375
- out_weight: bfloat16 [8192, 4096], P('tensor'), may hold values from -0.0625 to 0.0625
- past_cache: bfloat16 [1024, 64, 2, 1024], P('dp', None, None, 'tensor'), parts along dimension 0, may hold values from -320 to 320
- exponents: int32 [10240, 32], P('dp'), parts along dimension 0, may hold values from -11 to -7
Outputs:
- mixed: bfloat16 [10240, 4096], P(('dp', 'tensor')), parts along dimension 0
There are 8 independent parts, one for each index of `dp`. A program takes and returns all parts, laid end to end along the dimension named above; an argument that names none is the same for every part. Nothing has to cross between parts.
All inputs are finite; a program needn't handle non-finite values.
Results may differ from a plain program's by a relative error of at most 0.012.
The roundings to bfloat16 on the way count: a program that leaves them out, or rounds other values in their place, can miss the bound.
Values may be sent and summed in bfloat16 or wider, within the bound.
A program may use at most 192 MiB of HBM per device.

v0:
```python
import jax
import jax.numpy as jnp
from jax import lax
from jax.sharding import PartitionSpec as P

HD = 128
NEW = 10
CACHE = 64


epsilon = 1e-05
theta_base = 500000.0


def rotate(matrix, heads):
    row_count = matrix.shape[0]
    half_dim = HD // 2
    positions = (jnp.arange(row_count, dtype=jnp.int32) % NEW + CACHE).astype(jnp.float32)
    frequency = theta_base ** (-(jnp.arange(half_dim, dtype=jnp.float32) * 2.0) / HD)
    angles = positions[:, None] * frequency[None, :]
    cosine = jnp.cos(angles)[:, None, :]
    sine_part = jnp.sin(angles)[:, None, :]
    shaped = matrix.reshape(row_count, heads, 2, half_dim)
    first = shaped[:, :, 0]
    second = shaped[:, :, 1]
    turned = jnp.stack(
        [first * cosine - second * sine_part, second * cosine + first * sine_part], 2
    )
    return turned.reshape(row_count, heads * HD)


def attention(query, key_new, value_new, past_cache, kv_heads):
    row_count = query.shape[0]
    seq_count = row_count // NEW
    group_size = query.shape[1] // (kv_heads * HD)
    cache_len = past_cache.shape[1]
    query_heads = query.reshape(seq_count, NEW, kv_heads, group_size, HD)
    new_keys = key_new.reshape(seq_count, NEW, kv_heads, HD)
    new_values = value_new.reshape(seq_count, NEW, kv_heads, HD)
    cache_keys = past_cache[:, :, 0].reshape(seq_count, cache_len, kv_heads, HD)
    cache_values = past_cache[:, :, 1].reshape(seq_count, cache_len, kv_heads, HD)
    inv_root = 1.0 / HD**0.5
    cache_scores = (
        jnp.einsum("stkgd,sckd->skgtc", query_heads, cache_keys, preferred_element_type=jnp.float32)
        * inv_root
    )
    new_scores = (
        jnp.einsum("stkgd,sukd->skgtu", query_heads, new_keys, preferred_element_type=jnp.float32)
        * inv_root
    )
    causal = jnp.arange(NEW)[:, None] >= jnp.arange(NEW)[None, :]
    new_scores = jnp.where(causal, new_scores, -1e30)
    row_max = jnp.maximum(cache_scores.max(-1), new_scores.max(-1))[..., None]
    cache_probs = jnp.exp(cache_scores - row_max)
    new_probs = jnp.exp(new_scores - row_max)
    denominator = (cache_probs.sum(-1) + new_probs.sum(-1))[..., None]
    cache_weights = (cache_probs / denominator).astype(jnp.bfloat16)
    new_weights = (new_probs / denominator).astype(jnp.bfloat16)
    combined = jnp.einsum(
        "skgtc,sckd->stkgd", cache_weights, cache_values, preferred_element_type=jnp.float32
    )
    combined = combined + jnp.einsum(
        "skgtu,sukd->stkgd", new_weights, new_values, preferred_element_type=jnp.float32
    )
    return combined.reshape(row_count, kv_heads * group_size * HD).astype(jnp.bfloat16)


def on_device(
    tokens, norm_gain, query_weight, key_weight, value_weight, out_weight, past_cache, exponents
):
    kv_local = key_weight.shape[1] // HD
    query_local = query_weight.shape[1] // HD
    query_cols = query_weight.shape[1]
    key_cols = key_weight.shape[1]
    gain_f32 = norm_gain.astype(jnp.float32)
    floats = lax.all_gather(tokens, "tensor", axis=0, tiled=True).astype(jnp.float32)
    normed = floats * lax.rsqrt(jnp.mean(floats * floats, axis=-1, keepdims=True) + epsilon)
    normed = (normed * gain_f32).astype(jnp.bfloat16)
    projected = jnp.concatenate(
        [
            jnp.dot(normed, query_weight, preferred_element_type=jnp.float32),
            jnp.dot(normed, key_weight, preferred_element_type=jnp.float32),
            jnp.dot(normed, value_weight, preferred_element_type=jnp.float32),
        ],
        1,
    )
    query = rotate(projected[:, :query_cols], query_local).astype(jnp.bfloat16)
    key_new = rotate(projected[:, query_cols : query_cols + key_cols], kv_local).astype(
        jnp.bfloat16
    )
    value_new = projected[:, query_cols + key_cols :].astype(jnp.bfloat16)
    attended = attention(query, key_new, value_new, past_cache, kv_local)
    partial_value = jnp.dot(attended, out_weight, preferred_element_type=jnp.float32)
    row_count = partial_value.shape[0]
    groups = exponents.shape[1]
    shrink = jnp.exp2(-exponents.astype(jnp.float32))[..., None]
    scaled = jnp.clip(partial_value.reshape(row_count, groups, -1) * shrink, -127.0, 127.0)
    rounded = lax.optimization_barrier(scaled.astype(jnp.bfloat16)).astype(jnp.float32)
    rounded = rounded.reshape(row_count, -1)
    own_rows = row_count // lax.axis_size("tensor")
    share = lax.psum_scatter(
        rounded.astype(jnp.bfloat16), "tensor", scatter_dimension=0, tiled=True
    ).astype(jnp.float32)
    own_exponents = lax.dynamic_slice_in_dim(
        exponents, lax.axis_index("tensor") * own_rows, own_rows, 0
    )
    restore = jnp.exp2(own_exponents.astype(jnp.float32))[..., None]
    layer_out = tokens.astype(jnp.float32) + (
        share.reshape(own_rows, groups, -1) * restore
    ).reshape(own_rows, -1)
    return layer_out.astype(jnp.bfloat16)


def solution(mesh):
    return jax.shard_map(
        on_device,
        mesh=mesh,
        in_specs=(
            P(("dp", "tensor"), None),
            P(),
            P(None, "tensor"),
            P(None, "tensor"),
            P(None, "tensor"),
            P("tensor", None),
            P("dp", None, None, "tensor"),
            P("dp", None),
        ),
        out_specs=P(("dp", "tensor"), None),
        check_vma=False,
    )
```

profile of v0, /device:TPU:0, one launch (start us, length us, event | category | flops | bytes accessed | tf_op | source)
XLA Modules:
  0.0 529.3 jit_solution(1144618563011597819)
XLA Ops:
  6.5 0.0 copy-start
  6.5 0.0 all-gather.2.cloned.1.call-start
  6.5 0.7 all-gather.2.cloned.1.call-update
  7.3 0.0 reduce-scatter.4.cloned.1.call-start
  7.3 20.2 %fusion.30 = (bf16[128,64,1,256]{3,2,1,0:T(2,128)(2,1)}, bf16[128,64,1,256]{3,2,1,0:T(2,128)(2,1)}) fusion(bf16[128,64,2,256]{3,2,1,0:T(2,128)(2,1)} %param.14), kind=kLoop, calls=%fused_computation.54 | loop fusion | bytes 16777216 | tf_op jit(solution)/shard_map/slice | solution.py:40
  27.5 17.5 %copy.145 = bf16[128,64,1,256]{0,3,1,2:T(8,128)(2,1)} copy(bf16[128,64,1,256]{3,2,1,0:T(2,128)(2,1)} %get-tuple-element.8) | data formatting | bytes 8388608
  45.0 6.5 %copy.125 = bf16[128,64,2,128,1]{3,1,4,2,0:T(8,128)(2,1)} copy(bf16[128,64,2,128,1]{0,3,2,1,4:T(8,128)(2,1)} %bitcast.54) | data formatting | bytes 8388608 | tf_op jit(solution)/shard_map/reshape;squeeze | solution.py:41
  51.5 17.7 %copy.144 = bf16[128,64,1,256]{0,3,1,2:T(8,128)(2,1)} copy(bf16[128,64,1,256]{3,2,1,0:T(2,128)(2,1)} %get-tuple-element.7) | data formatting | bytes 8388608
  69.2 6.6 %copy.121 = bf16[128,64,2,128,1]{3,1,4,2,0:T(8,128)(2,1)} copy(bf16[128,64,2,128,1]{0,3,2,1,4:T(8,128)(2,1)} %bitcast.55) | data formatting | bytes 8388608 | tf_op jit(solution)/shard_map/reshape;squeeze | solution.py:40
  75.7 0.0 copy-done.6
  75.8 1.2 multiply_cosine_fusion
  77.0 1.1 copy.99
  78.1 1.1 copy.97
  79.2 22.6 %copy.137 = bf16[4096,2048]{1,0:T(8,128)(2,1)} copy(bf16[4096,2048]{0,1:T(8,128)(2,1)} %bitcast.56) | data formatting | bytes 33554432 | tf_op jit(solution)/shard_map/dot_general | solution.py:93
  101.8 0.0 copy-done.4
  101.8 0.7 multiply_exponential_fusion
  102.5 14.4 %all-gather.2.cloned.1.call-done = bf16[1280,4096]{1,0:T(8,128)(2,1)} async-done(((bf16[320,4096]{1,0:T(8,128)(2,1)}), bf16[1280,4096]{1,0:T(8,128)(2,1)}) %all-gather.2.cloned.1.call-update) | async-done | bytes 10485776 | tf_op jit(solution)/shard_map/all_gather | solution.py:76
  116.9 6.2 %fusion.1 = f32[1280]{0:T(1024)S(1)} fusion(bf16[1280,4096]{1,0:T(8,128)(2,1)} %all-gather.2.cloned.1.call-done), kind=kLoop, calls=%fused_computation.4 | loop fusion | flops 15727360 | bytes 10490880 | tf_op jit(solution)/shard_map/reduce_sum | solution.py:77
  123.1 0.7 copy-done.2
  123.8 30.1 %fusion.28 = f32[1280,2048]{0,1:T(8,128)} fusion(bf16[4096,2048]{1,0:T(8,128)(2,1)} %param.10, bf16[1280,4096]{1,0:T(8,128)(2,1)S(1)} %copy-done.2, f32[4096]{0:T(1024)S(1)} %convert_element_type.81, f32[1280]{0:T(1024)S(1)} %add_rsqrt_fusion), kind=kOutput, calls=%fused_computation.53 | convolution fusion | flops 21495808000 | bytes 37770240 | tf_op jit(solution)/shard_map/dot_general | solution.py:81
  153.9 4.8 subtract_convert_fusion
  158.8 2.7 pad_maximum_fusion
  161.5 21.9 %copy.92 = bf16[1280,16,2,64]{3,2,1,0:T(2,128)(2,1)} copy(bf16[1280,16,2,64]{0,3,2,1:T(8,128)(2,1)} %pad_maximum_fusion) | data formatting | bytes 10485760 | tf_op jit(solution)/shard_map/stack | solution.py:26
  183.4 17.5 %convert_element_type.84 = bf16[128,10,2,8,128]{4,3,2,1,0:T(8,128)(2,1)} reshape(bf16[1280,16,2,64]{3,2,1,0:T(2,128)(2,1)} %copy.92) | data formatting | bytes 10485760 | tf_op jit(solution)/shard_map/convert_element_type | solution.py:87
  200.9 11.9 %bitcast_reduce_fusion = (f32[128,2,8,10]{2,3,1,0:T(8,128)}, f32[128,2,10,8,64]{4,3,2,1,0:T(8,128)}) fusion(bf16[128,64,2,128,1]{3,1,4,2,0:T(8,128)(2,1)} %copy.121, bf16[128,10,2,8,128]{4,3,2,1,0:T(8,128)(2,1)} %convert_element_type.84), kind=kOutput, calls=%fused_computation.11 | convolution fusion | flops 338145280 | bytes 14761984 | tf_op jit(solution)/shard_map/stkgd,sckd->skgtc/dot_general | solution.py:44
  212.9 2.3 copy.104
  215.1 0.0 copy-done
  215.2 6.8 %fusion.26 = f32[1280,256]{0,1:T(8,128)S(1)} fusion(bf16[4096,256]{1,0:T(8,128)(2,1)S(1)} %copy-done, bf16[1280,4096]{1,0:T(8,128)(2,1)} %all-gather.2.cloned.1.call-done, f32[4096]{0:T(1024)S(1)} %convert_element_type.81, f32[1280]{0:T(1024)S(1)} %add_rsqrt_fusion), kind=kOutput, calls=%fused_computation.52 | convolution fusion | flops 2705326080 | bytes 13915136 | tf_op jit(solution)/shard_map/dot_general | solution.py:82
  222.0 0.0 copy-start.3
  222.0 0.9 fusion.31
  222.9 1.4 copy.143
  224.3 2.8 copy.142
  227.1 0.0 copy-done.3
  227.1 8.1 %subtract_convert_fusion.1 = (bf16[1280,2,1,64]{3,2,1,0:T(2,128)(2,1)S(1)}, bf16[1280,2,1,64]{3,2,1,0:T(2,128)(2,1)S(1)}) fusion(f32[1280,2,1,64]{3,2,1,0:T(1,128)S(1)} %copy.143, f32[1280,2,1,64]{3,2,1,0:T(1,128)S(1)} %copy.142, f32[1280,64]{1,0:T(8,128)S(1)} %copy-done.3, f32[1280,64]{1,0:T(8,128)} %copy.97), kind=kLoop, calls=%fused_computation.30 | loop fusion | flops 1310720 | bytes 2621440 | tf_op jit(solution)/shard_map/convert
  235.2 3.7 pad_maximum_fusion.1
  239.0 0.6 convert_element_type.85
  239.7 7.9 %fusion.12 = f32[128,2,10,10,8]{2,4,3,1,0:T(8,128)} fusion(bf16[128,10,2,8,128]{4,3,2,1,0:T(8,128)(2,1)} %convert_element_type.84, bf16[128,10,2,128,1]{3,2,1,0,4:T(2,128)(2,1)S(1)} %bitcast.60), kind=kOutput, calls=%fused_computation.23 | convolution fusion | flops 52428800 | bytes 6717440 | tf_op jit(solution)/shard_map/stkgd,sukd->skgtu/dot_general | solution.py:48
  247.6 6.1 %copy.102 = f32[128,2,10,10,8]{0,4,2,3,1:T(8,128)S(1)} copy(f32[128,2,10,10,8]{2,4,3,1,0:T(8,128)} %fusion.12) | data formatting | bytes 1638400 | tf_op jit(solution)/shard_map/stkgd,sukd->skgtu/dot_general | solution.py:48
  253.7 0.2 fusion.19
  253.9 1.8 copy.106
  255.7 0.3 fusion.18
  256.0 11.7 %fusion.7 = f32[128,2,8,10]{2,3,1,0:T(8,128)} fusion(f32[128,2,10,8,64]{4,3,2,1,0:T(8,128)} %get-tuple-element.16, f32[128,2,8,10]{2,3,1,0:T(8,128)S(1)} %copy.106), kind=kLoop, calls=%fused_computation.14 | loop fusion | flops 3911680 | bytes 5406720 | tf_op jit(solution)/shard_map/reduce_sum | solution.py:56
  267.7 2.3 copy.108
  269.9 2.8 copy.110
  272.7 0.3 divide_convert_fusion.1
  273.0 9.5 %divide_convert_fusion = bf16[128,2,8,10,64]{4,2,3,1,0:T(8,128)(2,1)} fusion(f32[128,2,10,8,64]{4,3,2,1,0:T(8,128)} %get-tuple-element.16, f32[128,2,8,10]{2,3,1,0:T(8,128)} %copy.110, f32[128,2,8,10]{2,3,1,0:T(8,128)S(1)} %copy.106), kind=kLoop, calls=%fused_computation.13 | loop fusion | flops 5242880 | bytes 8028160 | tf_op jit(solution)/shard_map/convert_element_type | solution.py:57
  282.5 14.4 %copy.115 = bf16[128,2,8,10,10]{4,3,2,1,0:T(8,128)(2,1)} copy(bf16[128,2,8,10,10]{0,2,4,3,1:T(8,128)(2,1)S(1)} %divide_convert_fusion.1) | data formatting | bytes 819200 | tf_op jit(solution)/shard_map/convert_element_type | solution.py:58
  296.9 7.6 %convolution_convert_fusion = bf16[1280,256]{1,0:T(8,128)(2,1)S(1)} fusion(bf16[4096,256]{1,0:T(8,128)(2,1)} %param.12, bf16[1280,4096]{1,0:T(8,128)(2,1)} %all-gather.2.cloned.1.call-done, f32[4096]{0:T(1024)S(1)} %convert_element_type.81, f32[1280]{0:T(1024)S(1)} %add_rsqrt_fusion), kind=kOutput, calls=%fused_computation.27 | convolution fusion | flops 2705653760 | bytes 13259776 | tf_op jit(solution)/shard_map/dot_general | solution.py:83
  304.5 0.2 reshape.114
  304.7 11.8 %fusion.8 = f32[128,2,8,10,128]{4,3,2,1,0:T(8,128)} fusion(bf16[128,64,2,128,1]{3,1,4,2,0:T(8,128)(2,1)} %copy.125, bf16[128,2,8,10,64]{4,2,3,1,0:T(8,128)(2,1)} %divide_convert_fusion), kind=kOutput, calls=%fused_computation.15 | convolution fusion | flops 335544320 | bytes 17301504 | tf_op jit(solution)/shard_map/skgtc,sckd->stkgd/dot_general | solution.py:59
  316.5 12.9 %fusion.4 = bf16[128,10,2,8,128]{4,1,3,2,0:T(8,128)(2,1)} fusion(f32[128,2,8,10,128]{4,3,2,1,0:T(8,128)} %fusion.8, bf16[128,2,8,10,10]{4,3,2,1,0:T(8,128)(2,1)} %copy.115, bf16[128,10,2,128,1]{3,2,1,0,4:T(2,128)(2,1)S(1)} %bitcast.59), kind=kOutput, calls=%fused_computation.8 | convolution fusion | flops 57671680 | bytes 16793600 | tf_op jit(solution)/shard_map/skgtu,sukd->stkgd/dot_general | solution.py:62
  329.4 8.4 %copy.116 = bf16[128,10,2,8,128]{4,3,2,1,0:T(8,128)(2,1)} copy(bf16[128,10,2,8,128]{4,1,3,2,0:T(8,128)(2,1)} %fusion.4) | data formatting | bytes 10485760 | tf_op jit(solution)/shard_map/convert_element_type | solution.py:65
  337.8 8.9 %reshape.119 = bf16[1280,2048,1]{1,0,2:T(8,128)(2,1)} reshape(bf16[128,10,2,8,128]{4,3,2,1,0:T(8,128)(2,1)} %copy.116) | data formatting | bytes 10485760 | tf_op jit(solution)/shard_map/convert_element_type | solution.py:65
  346.7 0.0 copy-done.5
  346.7 28.5 %fusion.5 = bf16[1280,32,128]{2,0,1:T(8,128)(2,1)} fusion(bf16[1280,2048,1]{1,0,2:T(8,128)(2,1)} %reshape.119, bf16[32,128,2048]{2,1,0:T(8,128)(2,1)} %bitcast.57, f32[1280,32]{0,1:T(8,128)S(1)} %copy-done.5), kind=kOutput, calls=%fused_computation.9 | convolution fusion | flops 21490565120 | bytes 32669696 | tf_op jit(solution)/shard_map/dot_general | solution.py:93
  375.2 14.5 %copy.118 = bf16[1280,32,128]{0,2,1:T(8,128)(2,1)} copy(bf16[1280,32,128]{2,0,1:T(8,128)(2,1)} %fusion.5) | data formatting | bytes 20971520 | tf_op jit(solution)/shard_map/optimization_barrier | solution.py:98
  389.7 14.3 %copy.138 = bf16[1280,4096]{1,0:T(8,128)(2,1)} copy(bf16[1280,4096]{0,1:T(8,128)(2,1)} %bitcast.53) | data formatting | bytes 20971520
  403.9 0.0 reduce-scatter.4.cloned.1.call-update
  404.0 4.6 copy.90
  408.6 0.9 multiply_exponential_fusion.1
  409.5 98.1 %reduce-scatter.4.cloned.1.call-done = bf16[320,4096]{1,0:T(8,128)(2,1)} async-done(((bf16[1280,4096]{1,0:T(8,128)(2,1)}), bf16[320,4096]{1,0:T(8,128)(2,1)}) %reduce-scatter.4.cloned.1.call-update) | async-done | bytes 2621456
  507.6 4.5 copy.139
  512.1 5.6 %fusion.11 = bf16[320,4096]{0,1:T(8,128)(2,1)} fusion(bf16[320,4096]{0,1:T(8,128)(2,1)} %copy.139, bf16[320,4096]{0,1:T(8,128)(2,1)} %copy.90, f32[320,32]{0,1:T(8,128)S(1)} %multiply_exponential_fusion.1), kind=kLoop, calls=%fused_computation.19 | loop fusion | flops 6553600 | bytes 7905280 | tf_op jit(solution)/shard_map/convert_element_type | solution.py:111
  517.7 4.5 copy.119
  (13 shorter events, 0.1 us)
Async XLA Ops:
  6.5 208.6 %copy-start = (bf16[4096,256]{1,0:T(8,128)(2,1)S(1)}, bf16[4096,256]{1,0:T(8,128)(2,1)}, u32[]{:S(2)}) copy-start(bf16[4096,256]{1,0:T(8,128)(2,1)} %param.11) | copy-start | bytes 6291460
  6.5 110.3 %all-gather.2.cloned.1.call-start = ((), (), s32[]{:S(2)}) async-start(), calls=%async_computation.1 | async-start | bytes 13107200 | tf_op jit(solution)/shard_map/all_gather | solution.py:76
  7.3 500.3 %reduce-scatter.4.cloned.1.call-start = ((), (), s32[]{:S(2)}) async-start(), calls=%async_computation.2 | async-start | bytes 13107200
  69.2 6.6 %copy-start.6 = (bf16[4096]{0:T(1024)(128)(2,1)S(1)}, bf16[4096]{0:T(1024)(128)(2,1)}, u32[]{:S(2)}) copy-start(bf16[4096]{0:T(1024)(128)(2,1)} %param.9) | copy-start | bytes 24580
  79.2 22.6 %copy-start.4 = (s32[1280,32]{0,1:T(8,128)S(1)}, s32[1280,32]{0,1:T(8,128)}, u32[]{:S(2)}) copy-start(s32[1280,32]{0,1:T(8,128)} %param.15) | copy-start | bytes 491524
  116.9 7.0 %copy-start.2 = (bf16[1280,4096]{1,0:T(8,128)(2,1)S(1)}, bf16[1280,4096]{1,0:T(8,128)(2,1)}, u32[]{:S(2)}) copy-start(bf16[1280,4096]{1,0:T(8,128)(2,1)} %all-gather.2.cloned.1.call-done) | copy-start | bytes 31457284
  222.0 5.1 copy-start.3
  337.8 8.9 %copy-start.5 = (f32[1280,32]{0,1:T(8,128)S(1)}, f32[1280,32]{0,1:T(8,128)}, u32[]{:S(2)}) copy-start(f32[1280,32]{0,1:T(8,128)} %multiply_exponential_fusion) | copy-start | bytes 491524
  512.1 10.1 %copy-start.1 = (bf16[4096,256]{1,0:T(8,128)(2,1)S(1)}, bf16[4096,256]{1,0:T(8,128)(2,1)}, u32[]{:S(2)}) copy-start(bf16[4096,256]{1,0:T(8,128)(2,1)} %param.11) | copy-start | bytes 6291460
Sparse Core Ops, SparseCore 0:
  9.2 107.6 all-gather.1
  404.1 103.4 reduce-scatter.3
where the time goes:
time: 538 us; the launch traced here: 529 us
  local copies, waits for them, and re-layouts  229 us (43%)
  matrix products  118 us (22%)
  waiting for transfers between devices  113 us (21%)
  other arithmetic  56 us (10%)
  between operations  13.8 us (3%)
    unnamed x3, waiting for transfers between devices  98.8 us
    unnamed x21, local copies, waits for them, and re-layouts  63.4 us
    dot_general x1, matrix products, on_device(): jnp.dot(normed, query_weight, preferred_element_type=jnp.float32)  30.1 us
    dot_general x1, matrix products, on_device(): jnp.dot(attended, out_weight, preferred_element_type=jnp.float32)  28.5 us
    dot_general x1, local copies, waits for them, and re-layouts, on_device(): jnp.dot(attended, out_weight, preferred_element_type=jnp.float32)  22.6 us
    another operation x1, local copies, waits for them, and re-layouts, rotate(): jnp.stack([first * cosine - second * sine_part, second * cosine + first *...  21.9 us
    slice x1, local copies, waits for them, and re-layouts, attention(): cache_keys = past_cache[:, :, 0].reshape(seq_count, cache_len, kv_heads, HD)  20.2 us
    convert_element_type x1, local copies, waits for them, and re-layouts, on_device(): query = rotate(projected[:, :query_cols], query_local).astype(jnp.bfloat16)  17.5 us
  transfers between devices with their start and end apart: 2, of which 2 were waited for; matrix products, arithmetic and copies ran while one was open for 19% of the time, Pallas kernels for 0%

commit v1 on v0

v1 whole, which is shorter than its diff:
```python
import functools

import jax
import jax.numpy as jnp
from jax import lax
from jax.experimental import pallas as pl
from jax.experimental.pallas import tpu as pltpu
from jax.sharding import PartitionSpec as P

HD = 128
NEW = 10
CHUNKS = 2
SEQ_BLOCK = 8

epsilon = 1e-05
theta_base = 500000.0


def rotary_tables(row_count):
    half_dim = HD // 2
    positions = (jnp.arange(row_count, dtype=jnp.int32) % NEW + 64).astype(jnp.float32)
    frequency = theta_base ** (-(jnp.arange(half_dim, dtype=jnp.float32) * 2.0) / HD)
    angles = positions[:, None] * frequency[None, :]
    cosine = jnp.cos(angles)
    sine_part = jnp.sin(angles)
    return (
        jnp.concatenate([cosine, cosine], 1),
        jnp.concatenate([-sine_part, sine_part], 1),
    )


def turn(block, cosine, sine_part):
    heads = []
    for h in range(block.shape[1] // HD):
        head = block[:, h * HD : (h + 1) * HD]
        heads.append(head * cosine + pltpu.roll(head, HD // 2, 1) * sine_part)
    return jnp.concatenate(heads, 1) if len(heads) > 1 else heads[0]


def project_kernel(x_ref, wq_ref, wk_ref, wv_ref, cos_ref, sin_ref, q_ref, k_ref, v_ref):
    normed = x_ref[...]
    cosine = cos_ref[...]
    sine_part = sin_ref[...]

    @pl.when(pl.program_id(0) == 0)
    def _():
        key = jnp.dot(normed, wk_ref[...], preferred_element_type=jnp.float32)
        k_ref[...] = turn(key, cosine, sine_part).astype(jnp.bfloat16)
        value = jnp.dot(normed, wv_ref[...], preferred_element_type=jnp.float32)
        v_ref[...] = value.astype(jnp.bfloat16)

    query = jnp.dot(normed, wq_ref[...], preferred_element_type=jnp.float32)
    q_ref[...] = turn(query, cosine, sine_part).astype(jnp.bfloat16)


def project(normed, query_weight, key_weight, value_weight, cosine, sine_part):
    rows, depth = normed.shape
    q_cols = query_weight.shape[1]
    k_cols = key_weight.shape[1]
    width = 512
    whole = lambda j: (0, 0)
    return pl.pallas_call(
        project_kernel,
        grid=(q_cols // width,),
        in_specs=[
            pl.BlockSpec((rows, depth), whole),
            pl.BlockSpec((depth, width), lambda j: (0, j)),
            pl.BlockSpec((depth, k_cols), whole),
            pl.BlockSpec((depth, k_cols), whole),
            pl.BlockSpec((rows, HD), whole),
            pl.BlockSpec((rows, HD), whole),
        ],
        out_specs=[
            pl.BlockSpec((rows, width), lambda j: (0, j)),
            pl.BlockSpec((rows, k_cols), whole),
            pl.BlockSpec((rows, k_cols), whole),
        ],
        out_shape=[
            jax.ShapeDtypeStruct((rows, q_cols), jnp.bfloat16),
            jax.ShapeDtypeStruct((rows, k_cols), jnp.bfloat16),
            jax.ShapeDtypeStruct((rows, k_cols), jnp.bfloat16),
        ],
        compiler_params=pltpu.CompilerParams(vmem_limit_bytes=56 * 1024 * 1024),
    )(normed, query_weight, key_weight, value_weight, cosine, sine_part)


def attend_kernel(kv_heads, group, q_ref, k_ref, v_ref, cache_ref, bias_ref, out_ref):
    rows = q_ref.shape[0]
    inv_root = 1.0 / HD**0.5
    bias = bias_ref[...]
    for kv in range(kv_heads):
        base = kv * group * HD
        query = jnp.concatenate(
            [q_ref[:, base + g * HD : base + (g + 1) * HD] for g in range(group)], 0
        )
        span = slice(kv * HD, (kv + 1) * HD)
        v_span = slice((kv_heads + kv) * HD, (kv_heads + kv + 1) * HD)
        keys = jnp.concatenate([cache_ref[:, span], k_ref[:, span]], 0)
        values = jnp.concatenate([cache_ref[:, v_span], v_ref[:, span]], 0)
        scores = lax.dot_general(
            query, keys, (((1,), (1,)), ((), ())), preferred_element_type=jnp.float32
        )
        weights = []
        for g in range(group):
            part = scores[g * rows : (g + 1) * rows] * inv_root + bias
            probs = jnp.exp(part - jnp.max(part, axis=-1, keepdims=True))
            scale = 1.0 / jnp.sum(probs, axis=-1, keepdims=True)
            weights.append((probs * scale).astype(jnp.bfloat16))
        combined = jnp.dot(
            jnp.concatenate(weights, 0), values, preferred_element_type=jnp.float32
        ).astype(jnp.bfloat16)
        for g in range(group):
            out_ref[:, base + g * HD : base + (g + 1) * HD] = combined[
                g * rows : (g + 1) * rows
            ]


def attend(query, key_new, value_new, cache, cache_len, ranks, chunk):
    rows, q_cols = query.shape
    k_cols = key_new.shape[1]
    kv_heads = k_cols // HD
    group = q_cols // k_cols
    block_rows = SEQ_BLOCK * NEW
    blocks = rows // block_rows
    per_rank = blocks // ranks
    cache_rows = SEQ_BLOCK * cache_len
    row_seq = jnp.arange(block_rows)[:, None] // NEW
    row_new = jnp.arange(block_rows)[:, None] % NEW
    in_cache = row_seq == jnp.arange(cache_rows)[None, :] // cache_len
    new_col = jnp.arange(block_rows)[None, :]
    in_new = (row_seq == new_col // NEW) & (row_new >= new_col % NEW)
    bias = jnp.where(jnp.concatenate([in_cache, in_new], 1), 0.0, -1e30).astype(jnp.float32)
    return pl.pallas_call(
        functools.partial(attend_kernel, kv_heads, group),
        grid=(blocks,),
        in_specs=[
            pl.BlockSpec((block_rows, q_cols), lambda i: (i, 0)),
            pl.BlockSpec((block_rows, k_cols), lambda i: (i, 0)),
            pl.BlockSpec((block_rows, k_cols), lambda i: (i, 0)),
            pl.BlockSpec(
                (cache_rows, 2 * k_cols),
                lambda i: (
                    (i // per_rank) * (per_rank * CHUNKS) + chunk * per_rank + i % per_rank,
                    0,
                ),
            ),
            pl.BlockSpec((block_rows, cache_rows + block_rows), lambda i: (0, 0)),
        ],
        out_specs=pl.BlockSpec((block_rows, q_cols), lambda i: (i, 0)),
        out_shape=jax.ShapeDtypeStruct((rows, q_cols), jnp.bfloat16),
        compiler_params=pltpu.CompilerParams(vmem_limit_bytes=56 * 1024 * 1024),
    )(query, key_new, value_new, cache, bias)


def out_kernel(group_cols, a_ref, w_ref, shrink_ref, out_ref):
    partial_value = jnp.dot(a_ref[...], w_ref[...], preferred_element_type=jnp.float32)
    for i in range(out_ref.shape[1] // group_cols):
        span = slice(i * group_cols, (i + 1) * group_cols)
        scaled = jnp.clip(partial_value[:, span] * shrink_ref[0, :, i : i + 1], -127.0, 127.0)
        out_ref[:, span] = scaled.astype(jnp.bfloat16)


def project_out(attended, out_weight, shrink):
    rows, depth = attended.shape
    cols = out_weight.shape[1]
    groups = shrink.shape[1]
    group_cols = cols // groups
    width = 512
    per_block = width // group_cols
    shrink = shrink.reshape(rows, groups // per_block, per_block).transpose(1, 0, 2)
    return pl.pallas_call(
        functools.partial(out_kernel, group_cols),
        grid=(cols // width,),
        in_specs=[
            pl.BlockSpec((rows, depth), lambda j: (0, 0)),
            pl.BlockSpec((depth, width), lambda j: (0, j)),
            pl.BlockSpec((1, rows, per_block), lambda j: (j, 0, 0)),
        ],
        out_specs=pl.BlockSpec((rows, width), lambda j: (0, j)),
        out_shape=jax.ShapeDtypeStruct((rows, cols), jnp.bfloat16),
        compiler_params=pltpu.CompilerParams(vmem_limit_bytes=56 * 1024 * 1024),
    )(attended, out_weight, shrink)


def on_device(
    tokens, norm_gain, query_weight, key_weight, value_weight, out_weight, past_cache, exponents
):
    own_rows, depth = tokens.shape
    ranks = lax.axis_size("tensor")
    step = own_rows // CHUNKS
    groups = exponents.shape[1]
    cache_len = past_cache.shape[1]
    gain_f32 = norm_gain.astype(jnp.float32)
    floats = tokens.astype(jnp.float32)
    gathered = []
    for c in range(CHUNKS):
        piece = floats[c * step : (c + 1) * step]
        normed = piece * lax.rsqrt(jnp.mean(piece * piece, axis=-1, keepdims=True) + epsilon)
        normed = (normed * gain_f32).astype(jnp.bfloat16)
        gathered.append(lax.all_gather(normed, "tensor", axis=0, tiled=True))
    cache = past_cache.reshape(past_cache.shape[0] * cache_len, -1)
    cosine, sine_part = rotary_tables(step * ranks)
    shrink = jnp.exp2(-exponents.astype(jnp.float32)).reshape(ranks, CHUNKS, step, groups)
    shares = []
    for c in range(CHUNKS):
        query, key_new, value_new = project(
            gathered[c], query_weight, key_weight, value_weight, cosine, sine_part
        )
        attended = attend(query, key_new, value_new, cache, cache_len, ranks, c)
        rounded = project_out(
            attended, out_weight, shrink[:, c].reshape(ranks * step, groups)
        )
        shares.append(lax.psum_scatter(rounded, "tensor", scatter_dimension=0, tiled=True))
    own_exponents = lax.dynamic_slice_in_dim(
        exponents, lax.axis_index("tensor") * own_rows, own_rows, 0
    )
    restore = jnp.exp2(own_exponents.astype(jnp.float32))
    outs = []
    for c in range(CHUNKS):
        span = slice(c * step, (c + 1) * step)
        wide = jnp.repeat(restore[span], depth // groups, axis=1)
        outs.append((floats[span] + shares[c].astype(jnp.float32) * wide).astype(jnp.bfloat16))
    return jnp.concatenate(outs, 0)


def solution(mesh):
    return jax.shard_map(
        on_device,
        mesh=mesh,
        in_specs=(
            P(("dp", "tensor"), None),
            P(),
            P(None, "tensor"),
            P(None, "tensor"),
            P(None, "tensor"),
            P("tensor", None),
            P("dp", None, None, "tensor"),
            P("dp", None),
        ),
        out_specs=P(("dp", "tensor"), None),
        check_vma=False,
    )
```

time: 538 us -> 286 us (0.53); the launches traced: 529 us -> 286 us
  local copies, waits for them, and re-layouts: 229 us -> 17.8 us
  Pallas kernels: 0 us -> 119 us
  matrix products: 118 us -> 0 us
  other arithmetic: 56 us -> 16.6 us
  waiting for transfers between devices: 113 us -> 119 us
    pallas_call x0 -> x6, Pallas kernels: none -> 119 us  [the longest x2 46 us: project(): pl.pallas_call(project_kernel, grid=(q_cols // width,), in_specs=[pl.Bloc...]
    dot_general x8 -> x0, matrix products: 118 us -> none  [the longest x1 30.1 us: on_device(): jnp.dot(normed, query_weight, preferred_element_type=jnp.float32)]
    unnamed x3 -> x4, waiting for transfers between devices: 98.8 us -> 0.74 us
    reduce_scatter x0 -> x2, waiting for transfers between devices: none -> 68.7 us  [on_device(): lax.psum_scatter(rounded, 'tensor', scatter_dimension=0, tiled=True)]
    convert_element_type x6 -> x0, local copies, waits for them, and re-layouts: 54.3 us -> none  [the longest x1 17.5 us: on_device(): query = rotate(projected[:, :query_cols], query_local).astype(jnp.bfloat16)]
    unnamed x21 -> x11, local copies, waits for them, and re-layouts: 63.4 us -> 10 us
    all_gather x1 -> x2, waiting for transfers between devices: 14.4 us -> 49.6 us  [on_device(): gathered.append(lax.all_gather(normed, 'tensor', axis=0, tiled=True))]
    another operation x3 -> x4, local copies, waits for them, and re-layouts: 35 us -> 4.94 us  [project_out(): shrink.reshape(rows, groups // per_block, per_block).transpose(1, 0, 2)]
  transfers between devices with their start and end apart: 2 -> 4, of which waited for: 2 -> 4; matrix products, arithmetic and copies ran while one was open for 19% -> 6% of each run, Pallas kernels for 0% -> 42%
where the time goes in v1:
time: 286 us
  waiting for transfers between devices  119 us (42%)
  Pallas kernels  119 us (42%)
  local copies, waits for them, and re-layouts  17.8 us (6%)
  other arithmetic  16.6 us (6%)
  between operations  13.3 us (5%)
    reduce_scatter x2, waiting for transfers between devices, on_device(): lax.psum_scatter(rounded, 'tensor', scatter_dimension=0, tiled=True)  68.7 us
    all_gather x2, waiting for transfers between devices, on_device(): gathered.append(lax.all_gather(normed, 'tensor', axis=0, tiled=True))  49.6 us
    pallas_call x2, Pallas kernels, project(): pl.pallas_call(project_kernel, grid=(q_cols // width,), in_specs=[pl.Bloc...  46 us
    pallas_call x2, Pallas kernels, attend(): pl.pallas_call(functools.partial(attend_kernel, kv_heads, group), grid=(b...  38.8 us
    pallas_call x2, Pallas kernels, project_out(): pl.pallas_call(functools.partial(out_kernel, group_cols), grid=(cols // w...  33.9 us
    unnamed x11, local copies, waits for them, and re-layouts  10 us
    convert_element_type x1, other arithmetic, on_device(): (floats[span] + shares[c].astype(jnp.float32) * wide).astype(jnp.bfloat16)  6.51 us
  transfers between devices with their start and end apart: 4, of which 4 were waited for; matrix products, arithmetic and copies ran while one was open for 6% of the time, Pallas kernels for 42%

profile of v1, /device:TPU:0, one launch (start us, length us, event | category | flops | bytes accessed | tf_op | source)
XLA Modules:
  0.0 285.7 jit_solution(15071269189751518112)
XLA Ops:
  6.5 0.0 all-gather.5.cloned.1.call-start
  6.5 2.4 convert_element_type.43
  8.9 0.0 copy-start
  8.9 0.0 copy-start.4
  8.9 0.4 multiply_reduce_fusion.1
  9.4 0.3 copy-done.4
  9.7 1.6 copy-done
  11.3 2.3 multiply_convert_fusion.1
  13.5 0.0 all-gather.5.cloned.1.call-update
  13.6 0.0 all-gather.3.cloned.1.call-start
  13.6 0.7 all-gather.3.cloned.1.call-update
  14.3 0.0 reduce-scatter.5.cloned.1.call-start
  14.4 0.0 copy-start.3
  14.4 8.1 %copy.19 = bf16[1024,8,2,256]{3,1,2,0:T(8,128)(2,1)} copy(bf16[1024,8,2,256]{3,2,1,0:T(2,128)(2,1)} %bitcast.31) | data formatting | bytes 16777216
  22.4 0.0 copy-done.3
  22.5 0.4 reshape.155
  22.9 0.8 slice_reduce_fusion.1
  23.6 0.2 reshape_reshape_squeeze.7
  23.8 2.3 copy.15
  26.2 0.1 compare_and_fusion
  26.3 0.1 broadcast_compare_fusion
  26.4 0.7 add_select_fusion.bias_ref
  27.1 1.2 fusion.4
  28.3 1.1 pad_maximum_fusion.1
  29.4 48.4 %all-gather.5.cloned.1.call-done.x_ref = bf16[640,4096]{1,0:T(8,128)(2,1)} async-done(((bf16[160,4096]{1,0:T(8,128)(2,1)}), bf16[640,4096]{1,0:T(8,128)(2,1)}) %all-gather.5.cloned.1.call-update) | async-done | bytes 5242896 | tf_op jit(solution)/shard_map/all_gather | solution.py:200
  77.8 23.0 %shard_map.85 = (bf16[640,2048]{1,0:T(8,128)(2,1)}, bf16[640,256]{1,0:T(8,128)(2,1)}, bf16[640,256]{1,0:T(8,128)(2,1)}) custom-call(bf16[640,4096]{1,0:T(8,128)(2,1)} %all-gather.5.cloned.1.call-done.x_ref, bf16[4096,2048]{1,0:T(8,128)(2,1)} %wq_ref.3, bf16[4096,256]{1,0:T(8,128)(2,1)} %wk_ref.3, bf16[4096,256]{1,0:T(8,128)(2,1)} %wv_ref.3, ...), custom_call_target="tpu_custom_call" | custom-call | tf_op jit(solution)/shard_map/pallas_call | solution.py:62
  100.7 19.4 %shard_map.86.a_ref = bf16[640,2048]{1,0:T(8,128)(2,1)} custom-call(bf16[640,2048]{1,0:T(8,128)(2,1)} %get-tuple-element.14.q_ref, bf16[640,256]{1,0:T(8,128)(2,1)} %get-tuple-element.15.k_ref, bf16[640,256]{1,0:T(8,128)(2,1)} %get-tuple-element.16.v_ref, bf16[8192,512]{1,0:T(8,128)(2,1)} %bitcast.25, f32[80,592]{1,0:T(8,128)} %add_select_fusion.bias_ref), custom_call_target="tpu_custom_call" | custom-call | tf_op jit(solution)/shard_map/pallas_call | solution.py:133
  120.1 16.9 %shard_map.87 = bf16[640,4096]{1,0:T(8,128)(2,1)} custom-call(bf16[640,2048]{1,0:T(8,128)(2,1)} %shard_map.86.a_ref, bf16[2048,4096]{1,0:T(8,128)(2,1)} %w_ref.3, f32[8,640,4]{2,1,0:T(8,128)} %bitcast.27), custom_call_target="tpu_custom_call" | custom-call | tf_op jit(solution)/shard_map/pallas_call | solution.py:171
  137.0 0.0 reduce-scatter.5.cloned.1.call-update
  137.0 0.2 reduce-scatter.3.cloned.1.call-start
  137.2 0.2 reshape_reshape_squeeze.6
  137.4 2.3 copy.12
  139.7 1.2 all-gather.3.cloned.1.call-done.x_ref
  140.9 23.0 %shard_map.82 = (bf16[640,2048]{1,0:T(8,128)(2,1)}, bf16[640,256]{1,0:T(8,128)(2,1)}, bf16[640,256]{1,0:T(8,128)(2,1)}) custom-call(bf16[640,4096]{1,0:T(8,128)(2,1)} %all-gather.3.cloned.1.call-done.x_ref, bf16[4096,2048]{1,0:T(8,128)(2,1)} %wq_ref.3, bf16[4096,256]{1,0:T(8,128)(2,1)} %wk_ref.3, bf16[4096,256]{1,0:T(8,128)(2,1)} %wv_ref.3, ...), custom_call_target="tpu_custom_call" | custom-call | tf_op jit(solution)/shard_map/pallas_call | solution.py:62
  164.0 19.4 %shard_map.83.a_ref = bf16[640,2048]{1,0:T(8,128)(2,1)} custom-call(bf16[640,2048]{1,0:T(8,128)(2,1)} %get-tuple-element.11.q_ref, bf16[640,256]{1,0:T(8,128)(2,1)} %get-tuple-element.12.k_ref, bf16[640,256]{1,0:T(8,128)(2,1)} %get-tuple-element.13.v_ref, bf16[8192,512]{1,0:T(8,128)(2,1)} %bitcast.26, f32[80,592]{1,0:T(8,128)} %add_select_fusion.bias_ref), custom_call_target="tpu_custom_call" | custom-call | tf_op jit(solution)/shard_map/pallas_call | solution.py:133
  183.4 17.0 %shard_map.84 = bf16[640,4096]{1,0:T(8,128)(2,1)} custom-call(bf16[640,2048]{1,0:T(8,128)(2,1)} %shard_map.83.a_ref, bf16[2048,4096]{1,0:T(8,128)(2,1)} %w_ref.3, f32[8,640,4]{2,1,0:T(8,128)} %bitcast.28), custom_call_target="tpu_custom_call" | custom-call | tf_op jit(solution)/shard_map/pallas_call | solution.py:171
  200.4 0.0 reduce-scatter.3.cloned.1.call-update
  200.4 0.1 multiply_exponential_fusion.1
  200.5 0.1 fusion.13
  200.6 0.1 copy.16
  200.7 0.1 copy.13
  200.8 4.5 %reduce-scatter.5.cloned.1.call-done = bf16[160,4096]{1,0:T(8,128)(2,1)} async-done(((bf16[640,4096]{1,0:T(8,128)(2,1)}), bf16[160,4096]{1,0:T(8,128)(2,1)}) %reduce-scatter.5.cloned.1.call-update) | async-done | bytes 1310736 | tf_op jit(solution)/shard_map/reduce_scatter | solution.py:213
  205.3 0.0 copy-start.1
  205.3 64.2 %reduce-scatter.3.cloned.1.call-done = bf16[160,4096]{1,0:T(8,128)(2,1)} async-done(((bf16[640,4096]{1,0:T(8,128)(2,1)}), bf16[160,4096]{1,0:T(8,128)(2,1)}) %reduce-scatter.3.cloned.1.call-update) | async-done | bytes 1310736 | tf_op jit(solution)/shard_map/reduce_scatter | solution.py:213
  269.5 0.0 copy-start.2
  269.5 0.7 broadcast_in_dim.17
  270.2 0.7 broadcast_in_dim.16
  271.0 0.0 copy-done.1
  271.0 0.0 copy-done.2
  271.0 6.5 %fusion.3 = (bf16[160,4096]{1,0:T(8,128)(2,1)S(1)}, bf16[160,4096]{1,0:T(8,128)(2,1)S(1)}) fusion(f32[20,8,32,128]{3,2,1,0:T(8,128)S(1)} %bitcast.30, bf16[160,4096]{1,0:T(8,128)(2,1)S(1)} %copy-done.2, f32[320,4096]{1,0:T(8,128)} %copy-done, f32[20,8,32,128]{3,2,1,0:T(8,128)S(1)} %bitcast.29, bf16[160,4096]{1,0:T(8,128)(2,1)S(1)} %copy-done.1), kind=kLoop, calls=%fused_computation.5 | loop fusion | flops 5242880 | bytes 15728640 | tf_op jit(solution)/shard_map/convert_element_type | solution.py:222
  277.5 1.7 pad_maximum_fusion
  (7 shorter events, 0.1 us)
Async XLA Ops:
  6.5 71.2 %all-gather.5.cloned.1.call-start = ((), (), s32[]{:S(2)}) async-start(), calls=%async_computation.4 | async-start | bytes 6553600 | tf_op jit(solution)/shard_map/all_gather | solution.py:200
  8.9 2.4 copy-start
  8.9 0.7 copy-start.4
  13.6 127.4 %all-gather.3.cloned.1.call-start = ((), (), s32[]{:S(2)}) async-start(), calls=%async_computation.2 | async-start | bytes 6553600 | tf_op jit(solution)/shard_map/all_gather | solution.py:200
  14.3 191.0 %reduce-scatter.5.cloned.1.call-start = ((), (), s32[]{:S(2)}) async-start(), calls=%async_computation.5 | async-start | bytes 6553600 | tf_op jit(solution)/shard_map/reduce_scatter | solution.py:213
  14.4 8.1 %copy-start.3 = (s32[1280,32]{0,1:T(8,128)S(1)}, s32[1280,32]{0,1:T(8,128)}, u32[]{:S(2)}) copy-start(s32[1280,32]{0,1:T(8,128)} %param.15) | copy-start | bytes 491524
  137.0 132.5 %reduce-scatter.3.cloned.1.call-start = ((), (), s32[]{:S(2)}) async-start(), calls=%async_computation.3 | async-start | bytes 6553600 | tf_op jit(solution)/shard_map/reduce_scatter | solution.py:213
  205.3 65.7 %copy-start.1 = (bf16[160,4096]{1,0:T(8,128)(2,1)S(1)}, bf16[160,4096]{1,0:T(8,128)(2,1)}, u32[]{:S(2)}) copy-start(bf16[160,4096]{1,0:T(8,128)(2,1)} %reduce-scatter.5.cloned.1.call-done) | copy-start | bytes 3932164
  269.5 1.5 copy-start.2
Sparse Core Ops, SparseCore 0:
  13.7 64.0 all-gather.4
  79.6 61.2 all-gather.2
  143.9 61.3 reduce-scatter.4
  208.1 61.3 reduce-scatter.2

commit v2 on v1

--- a/solution.py
+++ b/solution.py
@@ -182,6 +182,49 @@
     )(attended, out_weight, shrink)
 
 
+def norm_kernel(x_ref, gain_ref, out_ref):
+    floats = x_ref[...].astype(jnp.float32)
+    normed = floats * lax.rsqrt(jnp.mean(floats * floats, axis=-1, keepdims=True) + epsilon)
+    out_ref[...] = (normed * gain_ref[...].astype(jnp.float32)).astype(jnp.bfloat16)
+
+
+def normalise(tokens, gain, step, chunk):
+    depth = tokens.shape[1]
+    return pl.pallas_call(
+        norm_kernel,
+        grid=(1,),
+        in_specs=[
+            pl.BlockSpec((step, depth), lambda i: (chunk, 0)),
+            pl.BlockSpec((1, depth), lambda i: (0, 0)),
+        ],
+        out_specs=pl.BlockSpec((step, depth), lambda i: (0, 0)),
+        out_shape=jax.ShapeDtypeStruct((step, depth), jnp.bfloat16),
+    )(tokens, gain)
+
+
+def residual_kernel(tokens_ref, restore_ref, *refs):
+    out_ref = refs[-1]
+    start = 0
+    groups = restore_ref.shape[1]
+    width = tokens_ref.shape[1] // groups
+    for share_ref in refs[:-1]:
+        rows = slice(start, start + share_ref.shape[0])
+        start += share_ref.shape[0]
+        for g in range(groups):
+            cols = slice(g * width, (g + 1) * width)
+            term = share_ref[:, cols].astype(jnp.float32) * restore_ref[rows, g : g + 1]
+            out_ref[rows, cols] = (tokens_ref[rows, cols].astype(jnp.float32) + term).astype(
+                jnp.bfloat16
+            )
+
+
+def add_residual(tokens, shares, restore):
+    return pl.pallas_call(
+        residual_kernel,
+        out_shape=jax.ShapeDtypeStruct(tokens.shape, jnp.bfloat16),
+    )(tokens, restore, *shares)
+
+
 def on_device(
     tokens, norm_gain, query_weight, key_weight, value_weight, out_weight, past_cache, exponents
 ):
@@ -190,13 +233,9 @@
     step = own_rows // CHUNKS
     groups = exponents.shape[1]
     cache_len = past_cache.shape[1]
-    gain_f32 = norm_gain.astype(jnp.float32)
-    floats = tokens.astype(jnp.float32)
     gathered = []
     for c in range(CHUNKS):
-        piece = floats[c * step : (c + 1) * step]
-        normed = piece * lax.rsqrt(jnp.mean(piece * piece, axis=-1, keepdims=True) + epsilon)
-        normed = (normed * gain_f32).astype(jnp.bfloat16)
+        normed = normalise(tokens, norm_gain.reshape(1, depth), step, c)
         gathered.append(lax.all_gather(normed, "tensor", axis=0, tiled=True))
     cache = past_cache.reshape(past_cache.shape[0] * cache_len, -1)
     cosine, sine_part = rotary_tables(step * ranks)
@@ -215,12 +254,7 @@
         exponents, lax.axis_index("tensor") * own_rows, own_rows, 0
     )
     restore = jnp.exp2(own_exponents.astype(jnp.float32))
-    outs = []
-    for c in range(CHUNKS):
-        span = slice(c * step, (c + 1) * step)
-        wide = jnp.repeat(restore[span], depth // groups, axis=1)
-        outs.append((floats[span] + shares[c].astype(jnp.float32) * wide).astype(jnp.bfloat16))
-    return jnp.concatenate(outs, 0)
+    return add_residual(tokens, shares, restore)
 
 
 def solution(mesh):

time: 286 us -> 280 us (0.979)
  other arithmetic: 16.6 us -> 4.02 us
  Pallas kernels: 119 us -> 131 us
  waiting for transfers between devices: 119 us -> 115 us
    pallas_call x0 -> x3, Pallas kernels: none -> 11.9 us  [the longest x2 6.3 us: normalise(): pl.pallas_call(norm_kernel, grid=(1,), in_specs=[pl.BlockSpec((step, dept...]
    convert_element_type x4 -> x0, other arithmetic: 11.1 us -> none  [the longest x1 6.51 us: on_device(): (floats[span] + shares[c].astype(jnp.float32) * wide).astype(jnp.bfloat16)]
    all_gather x2, waiting for transfers between devices: 49.6 us -> 46.5 us  [on_device(): gathered.append(lax.all_gather(normed, 'tensor', axis=0, tiled=True))]
    unnamed x11 -> x4, local copies, waits for them, and re-layouts: 10 us -> 8.77 us
  transfers between devices with their start and end apart: 4 -> 4, of which waited for: 4 -> 4; matrix products, arithmetic and copies ran while one was open for 6% -> 7% of each run, Pallas kernels for 42% -> 44%
where the time goes in v2:
time: 280 us; the launch traced here: 279 us
  Pallas kernels  131 us (47%)
  waiting for transfers between devices  115 us (41%)
  local copies, waits for them, and re-layouts  16.2 us (6%)
  between operations  13.2 us (5%)
  other arithmetic  4.02 us (1%)
    reduce_scatter x2, waiting for transfers between devices, on_device(): lax.psum_scatter(rounded, 'tensor', scatter_dimension=0, tiled=True)  68.2 us
    all_gather x2, waiting for transfers between devices, on_device(): gathered.append(lax.all_gather(normed, 'tensor', axis=0, tiled=True))  46.5 us
    pallas_call x2, Pallas kernels, project(): pl.pallas_call(project_kernel, grid=(q_cols // width,), in_specs=[pl.Bloc...  46 us
    pallas_call x2, Pallas kernels, attend(): pl.pallas_call(functools.partial(attend_kernel, kv_heads, group), grid=(b...  38.7 us
    pallas_call x2, Pallas kernels, project_out(): pl.pallas_call(functools.partial(out_kernel, group_cols), grid=(cols // w...  33.9 us
    unnamed x4, local copies, waits for them, and re-layouts  8.77 us
    pallas_call x2, Pallas kernels, normalise(): pl.pallas_call(norm_kernel, grid=(1,), in_specs=[pl.BlockSpec((step, dept...  6.3 us
    pallas_call x1, Pallas kernels, add_residual(): pl.pallas_call(residual_kernel, out_shape=jax.ShapeDtypeStruct(tokens.sha...  5.61 us
  transfers between devices with their start and end apart: 4, of which 4 were waited for; matrix products, arithmetic and copies ran while one was open for 7% of the time, Pallas kernels for 44%

profile of v2, /device:TPU:0, one launch (start us, length us, event | category | flops | bytes accessed | tf_op | source)
XLA Modules:
  0.0 279.0 jit_solution(15868129733131798306)
XLA Ops:
  6.5 0.0 all-gather.5.cloned.1.call-start
  6.5 1.3 reshape.135.gain_ref
  7.8 3.1 %shard_map.86 = bf16[160,4096]{1,0:T(8,128)(2,1)} custom-call(bf16[320,4096]{1,0:T(8,128)(2,1)} %tokens_ref.1, bf16[1,4096]{1,0:T(2,128)(2,1)} %reshape.135.gain_ref), custom_call_target="tpu_custom_call" | custom-call | tf_op jit(solution)/shard_map/pallas_call | solution.py:193
  10.9 0.0 all-gather.5.cloned.1.call-update
  11.0 0.0 all-gather.3.cloned.1.call-start
  11.0 3.2 %shard_map.82 = bf16[160,4096]{1,0:T(8,128)(2,1)} custom-call(bf16[320,4096]{1,0:T(8,128)(2,1)} %tokens_ref.1, bf16[1,4096]{1,0:T(2,128)(2,1)} %reshape.135.gain_ref), custom_call_target="tpu_custom_call" | custom-call | tf_op jit(solution)/shard_map/pallas_call | solution.py:193
  14.2 0.0 all-gather.3.cloned.1.call-update
  14.2 0.0 reduce-scatter.5.cloned.1.call-start
  14.3 0.0 copy-start
  14.3 8.7 %copy.18 = bf16[1024,8,2,256]{3,1,2,0:T(8,128)(2,1)} copy(bf16[1024,8,2,256]{3,2,1,0:T(2,128)(2,1)} %bitcast.15) | data formatting | bytes 16777216
  23.0 0.0 copy-done
  23.0 0.4 reshape.137
  23.4 0.8 slice_reduce_fusion
  24.2 0.2 reshape_reshape_squeeze.7
  24.3 2.3 copy.14
  26.6 0.1 compare_and_fusion
  26.7 0.1 broadcast_compare_fusion
  26.8 0.7 add_select_fusion.bias_ref
  27.5 1.2 fusion
  28.7 1.2 pad_maximum_fusion
  29.9 45.2 %all-gather.5.cloned.1.call-done.x_ref = bf16[640,4096]{1,0:T(8,128)(2,1)} async-done(((bf16[160,4096]{1,0:T(8,128)(2,1)}), bf16[640,4096]{1,0:T(8,128)(2,1)}) %all-gather.5.cloned.1.call-update) | async-done | bytes 5242896 | tf_op jit(solution)/shard_map/all_gather | solution.py:239
  75.2 23.0 %shard_map.87 = (bf16[640,2048]{1,0:T(8,128)(2,1)}, bf16[640,256]{1,0:T(8,128)(2,1)}, bf16[640,256]{1,0:T(8,128)(2,1)}) custom-call(bf16[640,4096]{1,0:T(8,128)(2,1)} %all-gather.5.cloned.1.call-done.x_ref, bf16[4096,2048]{1,0:T(8,128)(2,1)} %wq_ref.3, bf16[4096,256]{1,0:T(8,128)(2,1)} %wk_ref.3, bf16[4096,256]{1,0:T(8,128)(2,1)} %wv_ref.3, ...), custom_call_target="tpu_custom_call" | custom-call | tf_op jit(solution)/shard_map/pallas_call | solution.py:62
  98.1 19.4 %shard_map.88.a_ref = bf16[640,2048]{1,0:T(8,128)(2,1)} custom-call(bf16[640,2048]{1,0:T(8,128)(2,1)} %get-tuple-element.14.q_ref, bf16[640,256]{1,0:T(8,128)(2,1)} %get-tuple-element.15.k_ref, bf16[640,256]{1,0:T(8,128)(2,1)} %get-tuple-element.16.v_ref, bf16[8192,512]{1,0:T(8,128)(2,1)} %bitcast.11, f32[80,592]{1,0:T(8,128)} %add_select_fusion.bias_ref), custom_call_target="tpu_custom_call" | custom-call | tf_op jit(solution)/shard_map/pallas_call | solution.py:133
  117.5 16.9 %shard_map.89 = bf16[640,4096]{1,0:T(8,128)(2,1)} custom-call(bf16[640,2048]{1,0:T(8,128)(2,1)} %shard_map.88.a_ref, bf16[2048,4096]{1,0:T(8,128)(2,1)} %w_ref.3, f32[8,640,4]{2,1,0:T(8,128)} %bitcast.13), custom_call_target="tpu_custom_call" | custom-call | tf_op jit(solution)/shard_map/pallas_call | solution.py:171
  134.4 0.0 reduce-scatter.5.cloned.1.call-update
  134.4 0.2 reduce-scatter.3.cloned.1.call-start
  134.6 0.2 reshape_reshape_squeeze.6
  134.8 2.3 copy.12
  137.1 1.3 all-gather.3.cloned.1.call-done.x_ref
  138.3 23.0 %shard_map.83 = (bf16[640,2048]{1,0:T(8,128)(2,1)}, bf16[640,256]{1,0:T(8,128)(2,1)}, bf16[640,256]{1,0:T(8,128)(2,1)}) custom-call(bf16[640,4096]{1,0:T(8,128)(2,1)} %all-gather.3.cloned.1.call-done.x_ref, bf16[4096,2048]{1,0:T(8,128)(2,1)} %wq_ref.3, bf16[4096,256]{1,0:T(8,128)(2,1)} %wk_ref.3, bf16[4096,256]{1,0:T(8,128)(2,1)} %wv_ref.3, ...), custom_call_target="tpu_custom_call" | custom-call | tf_op jit(solution)/shard_map/pallas_call | solution.py:62
  161.3 19.4 %shard_map.84.a_ref = bf16[640,2048]{1,0:T(8,128)(2,1)} custom-call(bf16[640,2048]{1,0:T(8,128)(2,1)} %get-tuple-element.11.q_ref, bf16[640,256]{1,0:T(8,128)(2,1)} %get-tuple-element.12.k_ref, bf16[640,256]{1,0:T(8,128)(2,1)} %get-tuple-element.13.v_ref, bf16[8192,512]{1,0:T(8,128)(2,1)} %bitcast.12, f32[80,592]{1,0:T(8,128)} %add_select_fusion.bias_ref), custom_call_target="tpu_custom_call" | custom-call | tf_op jit(solution)/shard_map/pallas_call | solution.py:133
  180.7 17.0 %shard_map.85 = bf16[640,4096]{1,0:T(8,128)(2,1)} custom-call(bf16[640,2048]{1,0:T(8,128)(2,1)} %shard_map.84.a_ref, bf16[2048,4096]{1,0:T(8,128)(2,1)} %w_ref.3, f32[8,640,4]{2,1,0:T(8,128)} %bitcast.14), custom_call_target="tpu_custom_call" | custom-call | tf_op jit(solution)/shard_map/pallas_call | solution.py:171
  197.7 0.0 reduce-scatter.3.cloned.1.call-update
  197.7 0.1 constant_dynamic-slice_fusion
  197.8 0.1 copy.15
  197.9 0.7 multiply_exponential_fusion.1.restore_ref
  198.6 4.0 %reduce-scatter.5.cloned.1.call-done.refs_1_ = bf16[160,4096]{1,0:T(8,128)(2,1)} async-done(((bf16[640,4096]{1,0:T(8,128)(2,1)}), bf16[160,4096]{1,0:T(8,128)(2,1)}) %reduce-scatter.5.cloned.1.call-update) | async-done | bytes 1310736 | tf_op jit(solution)/shard_map/reduce_scatter | solution.py:252
  202.7 64.2 %reduce-scatter.3.cloned.1.call-done.refs_0_ = bf16[160,4096]{1,0:T(8,128)(2,1)} async-done(((bf16[640,4096]{1,0:T(8,128)(2,1)}), bf16[160,4096]{1,0:T(8,128)(2,1)}) %reduce-scatter.3.cloned.1.call-update) | async-done | bytes 1310736 | tf_op jit(solution)/shard_map/reduce_scatter | solution.py:252
  266.9 5.6 %shard_map.90 = bf16[320,4096]{1,0:T(8,128)(2,1)} custom-call(bf16[320,4096]{1,0:T(8,128)(2,1)} %tokens_ref.1, f32[320,32]{1,0:T(8,128)} %multiply_exponential_fusion.1.restore_ref, bf16[160,4096]{1,0:T(8,128)(2,1)} %reduce-scatter.3.cloned.1.call-done.refs_0_, bf16[160,4096]{1,0:T(8,128)(2,1)} %reduce-scatter.5.cloned.1.call-done.refs_1_), custom_call_target="tpu_custom_call" | custom-call | tf_op jit(solution)/shard_map/pallas_call | solution.py:222
  (5 shorter events, 0.1 us)
Async XLA Ops:
  6.5 68.6 %all-gather.5.cloned.1.call-start = ((), (), s32[]{:S(2)}) async-start(), calls=%async_computation.4 | async-start | bytes 6553600 | tf_op jit(solution)/shard_map/all_gather | solution.py:239
  11.0 127.4 %all-gather.3.cloned.1.call-start = ((), (), s32[]{:S(2)}) async-start(), calls=%async_computation.2 | async-start | bytes 6553600 | tf_op jit(solution)/shard_map/all_gather | solution.py:239
  14.2 188.4 %reduce-scatter.5.cloned.1.call-start = ((), (), s32[]{:S(2)}) async-start(), calls=%async_computation.5 | async-start | bytes 6553600 | tf_op jit(solution)/shard_map/reduce_scatter | solution.py:252
  14.3 8.7 %copy-start = (s32[1280,32]{0,1:T(8,128)S(1)}, s32[1280,32]{0,1:T(8,128)}, u32[]{:S(2)}) copy-start(s32[1280,32]{0,1:T(8,128)} %param.15) | copy-start | bytes 491524
  134.4 132.5 %reduce-scatter.3.cloned.1.call-start = ((), (), s32[]{:S(2)}) async-start(), calls=%async_computation.3 | async-start | bytes 6553600 | tf_op jit(solution)/shard_map/reduce_scatter | solution.py:252
Sparse Core Ops, SparseCore 0:
  11.1 64.0 all-gather.4
  77.0 61.2 all-gather.2
  141.3 61.3 reduce-scatter.4
  205.5 61.3 reduce-scatter.2
